TPU v7x, 256 devices: a whole 4x4x8 slice. The times are simulated.
256 devices in a mesh: grp: 16 (over y, x), ep: 16 (over z, core).
Axes of the slice: x: 4, y: 4, z: 8, core: 2. Of those that a mesh axis runs over, the one named last changes fastest.
Arguments:
- tokens: bfloat16 [24576, 4096], P(('grp', 'ep')), may hold values from -6 to 6
- hash_expert: int32 [24576, 1], P(('grp', 'ep')), may hold values from 0 to 15, as said below
- gate_weight: bfloat16 [16, 4096, 4096], P('ep', None, 'grp'), may hold values from -0.09375 to 0.09375
- up_weight: bfloat16 [16, 4096, 4096], P('ep', None, 'grp'), may hold values from -0.09375 to 0.09375
- down_weight: bfloat16 [16, 4096, 4096], P('ep', 'grp'), may hold values from -0.09375 to 0.09375
Outputs:
- combined: bfloat16 [24576, 4096], P(('grp', 'ep'))
- expert_load: float32 [16], replicated
- balance: float32 [], replicated
Inputs may be any that keep to these rules, and one draw needn't show every extreme that they name: `hash_expert`: among the 96 rows of one device no expert is named more than 9 times; on every device some expert is named exactly 9 times; every expert is named by some row.
All inputs are finite; a program needn't handle non-finite values.
Results may differ from a plain program's by a relative error of at most 0.014.
Values may be sent and summed in bfloat16 or wider, within the bound.
A program may use at most 128 MiB of HBM per device.

v0:
```python
import jax
import jax.numpy as jnp
from jax import lax
from jax.sharding import Mesh
from jax.sharding import PartitionSpec as P

EP = ("ep_0", "ep_1")
GRP = ("grp_0", "grp_1")
GRP_EP = ("grp_0", "grp_1", "ep_0", "ep_1")
eps = 1e-06


def one_axis_at_a_time(array, axes):
    for axis in axes:
        array = lax.psum(array, axis)
    return array


def body(tokens, hash_expert, gate_weight, up_weight, down_weight):
    tok_dev, model_width = tokens.shape
    local_experts = gate_weight.shape[0]
    ep_size = lax.axis_size(EP)
    grp_size = lax.axis_size(GRP)
    experts = local_experts * ep_size
    capacity = max(2, 3 * tok_dev // (2 * experts))
    raw_values = tokens.astype(jnp.float32)
    normed = (
        raw_values * lax.rsqrt(jnp.mean(raw_values * raw_values, axis=-1, keepdims=True) + eps)
    ).astype(jnp.bfloat16)
    expert = hash_expert[:, 0]
    onehot = expert[:, None] == jnp.arange(experts, dtype=jnp.int32)[None, :]
    onehot_int = onehot.astype(jnp.int32)
    slot_index = jnp.sum((jnp.cumsum(onehot_int, axis=0) - 1) * onehot_int, axis=1)
    target = expert * capacity + slot_index
    placing = (jnp.arange(experts * capacity, dtype=jnp.int32)[:, None] == target[None, :]).astype(
        jnp.bfloat16
    )
    packed = jnp.dot(placing, normed, preferred_element_type=jnp.float32).astype(jnp.bfloat16)
    packed = packed.reshape(ep_size, local_experts, capacity, model_width)
    received = lax.all_to_all(packed, EP, split_axis=0, concat_axis=0, tiled=True)
    block_rows = lax.all_gather(received, GRP, axis=0, tiled=True)
    gate_out = jnp.einsum(
        "secd,edf->secf", block_rows, gate_weight, preferred_element_type=jnp.float32
    )
    up_out = jnp.einsum("secd,edf->secf", block_rows, up_weight, preferred_element_type=jnp.float32)
    hidden = (jax.nn.silu(gate_out) * up_out).astype(jnp.bfloat16)
    summed = lax.psum_scatter(
        jnp.einsum(
            "secf,efd->secd", hidden, down_weight, preferred_element_type=jnp.float32
        ).astype(jnp.bfloat16),
        GRP,
        scatter_dimension=0,
        tiled=True,
    )
    returned_rows = lax.all_to_all(summed, EP, split_axis=0, concat_axis=1, tiled=True)
    returned = returned_rows.reshape(experts * capacity, model_width)
    combined = jnp.dot(placing.T, returned, preferred_element_type=jnp.float32).astype(jnp.bfloat16)
    counts = one_axis_at_a_time(jnp.sum(onehot.astype(jnp.float32), axis=0), GRP_EP)
    expert_load = counts * experts / (tok_dev * grp_size * ep_size)
    balance = jnp.sum(expert_load * expert_load) / experts
    return (combined, expert_load, balance)


def solution(mesh):
    split = Mesh(mesh.devices.reshape(4, 4, 8, 2), ("grp_0", "grp_1", "ep_0", "ep_1"))
    placed = (
        P(GRP_EP, None),
        P(GRP_EP, None),
        P(EP, None, GRP),
        P(EP, None, GRP),
        P(EP, GRP, None),
    )
    return jax.shard_map(
        body, mesh=split, in_specs=placed, out_specs=(P(GRP_EP, None), P(), P()), check_vma=False
    )
```

profile of v0, /device:TPU:1, one launch (start us, length us, event | category | flops | bytes accessed | tf_op | source)
XLA Modules:
  0.0 449.0 jit_solution(12240543204433801340)
XLA Ops:
  7.2 0.0 copy-start
  7.2 0.0 all-gather.2.cloned.1.call-start
  7.2 0.9 fusion.25
  8.1 0.1 reduce_window_sum.11
  8.2 0.8 select_reduce_fusion
  9.1 0.7 multiply_add_fusion
  9.7 1.4 fusion.11
  11.2 1.7 convolution_convert_fusion
  12.8 1.6 reshape.52
  14.5 60.9 %all_to_all.14 = bf16[16,1,9,4096]{3,2,1,0:T(8,128)(2,1)S(1)} all-to-all(bf16[16,1,9,4096]{3,2,1,0:T(8,128)(2,1)} %bitcast.69), channel_id=1, replica_groups=mesh['grp_0'=4,'grp_1'=4,'ep_0'=8,'ep_1'=2] {'ep_0','ep_1'}, dimensions={0} | all-to-all | bytes 2359296 | tf_op jit(solution)/shard_map/all_to_all | solution.py:40
  75.3 1.8 copy.12
  77.1 0.0 all-gather.2.cloned.1.call-update
  77.1 0.0 reduce-scatter.2.cloned.1.call-start
  77.2 123.7 %all-gather.2.cloned.1.call-done = bf16[256,1,9,4096]{3,0,2,1:T(8,128)(2,1)} async-done(((bf16[16,1,9,4096]{3,0,2,1:T(8,128)(2,1)}), bf16[256,1,9,4096]{3,0,2,1:T(8,128)(2,1)}) %all-gather.2.cloned.1.call-update) | async-done | bytes 18874384 | tf_op jit(solution)/shard_map/all_gather | solution.py:41
  200.8 10.6 %fusion = f32[256,9,256]{2,0,1:T(8,128)} fusion(bf16[256,1,9,4096]{3,0,2,1:T(8,128)(2,1)} %all-gather.2.cloned.1.call-done, bf16[1,4096,256]{2,1,0:T(8,128)(2,1)} %param.8), kind=kOutput, calls=%fused_computation | convolution fusion | flops 4831838208 | bytes 23330816 | tf_op jit(solution)/shard_map/secd,edf->secf/dot_general | solution.py:45
  211.4 0.0 copy-done
  211.4 26.2 %convert_bitcast_fusion = bf16[256,1,9,4096]{3,0,2,1:T(8,128)(2,1)} fusion(bf16[1,256,4096]{2,1,0:T(8,128)(2,1)S(1)} %copy-done, f32[256,9,256]{2,0,1:T(8,128)} %fusion, bf16[256,1,9,4096]{3,0,2,1:T(8,128)(2,1)} %all-gather.2.cloned.1.call-done, bf16[1,4096,256]{2,1,0:T(8,128)(2,1)} %param.7), kind=kOutput, calls=%fused_computation.4 | convolution fusion | flops 9676652544 | bytes 44302336 | tf_op jit(solution)/shard_map/secf,efd->secd/dot_general | solution.py:48
  237.6 0.0 reduce-scatter.2.cloned.1.call-update
  237.6 125.7 %reduce-scatter.2.cloned.1.call-done = bf16[16,1,9,4096]{3,0,2,1:T(8,128)(2,1)} async-done(((bf16[256,1,9,4096]{3,0,2,1:T(8,128)(2,1)}), bf16[16,1,9,4096]{3,0,2,1:T(8,128)(2,1)}) %reduce-scatter.2.cloned.1.call-update) | async-done | bytes 1179664 | tf_op jit(solution)/shard_map/reduce_scatter | solution.py:47
  363.3 3.4 copy.13
  366.7 0.0 copy-start.1
  366.7 8.3 %all-to-all-start.1 = ((bf16[16,1,9,4096]{3,2,1,0:T(8,128)(2,1)}), bf16[16,1,9,4096]{3,2,1,0:T(8,128)(2,1)}, u32[]{:S(2)}, u32[]{:S(2)}) async-start(bf16[16,1,9,4096]{3,2,1,0:T(8,128)(2,1)} %copy.13), calls=%async_computation.2 | async-start | bytes 4194304 | tf_op jit(solution)/shard_map/all_to_all | solution.py:55
  375.0 0.0 copy-done.1
  375.0 0.1 convert_reduce_fusion
  375.1 8.8 %psum.28 = f32[16]{0:T(128)S(1)} all-reduce(f32[16]{0:T(128)S(1)} %convert_reduce_fusion), channel_id=1, replica_groups=mesh['grp_0'=4,'grp_1'=4,'ep_0'=8,'ep_1'=2] {'grp_0'}, use_global_device_ids=true, to_apply=%region_5.6 | all-reduce | flops 16 | bytes 128 | tf_op jit(solution)/shard_map/psum | solution.py:15
  383.9 7.4 %psum.29 = f32[16]{0:T(128)S(1)} all-reduce(f32[16]{0:T(128)S(1)} %psum.28), channel_id=1, replica_groups=mesh['grp_0'=4,'grp_1'=4,'ep_0'=8,'ep_1'=2] {'grp_1'}, use_global_device_ids=true, to_apply=%region_6.7 | all-reduce | flops 16 | bytes 128 | tf_op jit(solution)/shard_map/psum | solution.py:15
  391.3 39.3 %psum.30 = f32[16]{0:T(128)S(1)} all-reduce(f32[16]{0:T(128)S(1)} %psum.29), channel_id=1, replica_groups=mesh['grp_0'=4,'grp_1'=4,'ep_0'=8,'ep_1'=2] {'ep_0'}, use_global_device_ids=true, to_apply=%region_7.8 | all-reduce | flops 16 | bytes 128 | tf_op jit(solution)/shard_map/psum | solution.py:15
  430.6 5.5 %psum.31 = f32[16]{0:T(128)S(1)} all-reduce(f32[16]{0:T(128)S(1)} %psum.30), channel_id=1, replica_groups=mesh['grp_0'=4,'grp_1'=4,'ep_0'=8,'ep_1'=2] {'ep_1'}, use_global_device_ids=true, to_apply=%region_8.9 | all-reduce | flops 16 | bytes 128 | tf_op jit(solution)/shard_map/psum | solution.py:15
  436.1 1.1 multiply_reduce_fusion
  437.9 0.0 all-to-all-done.1
  437.9 1.8 reshape.58
  439.7 1.3 convolution_convert_fusion.1
  (1 shorter events, 0.0 us)
Async XLA Ops:
  7.2 204.3 %copy-start = (bf16[1,256,4096]{2,1,0:T(8,128)(2,1)S(1)}, bf16[1,256,4096]{2,1,0:T(8,128)(2,1)}, u32[]{:S(2)}) copy-start(bf16[1,256,4096]{2,1,0:T(8,128)(2,1)} %param.9) | copy-start | bytes 6291460
  7.2 193.7 %all-gather.2.cloned.1.call-start = ((), (), s32[]{:S(2)}) async-start(), calls=%async_computation.3 | async-start | bytes 20054016 | tf_op jit(solution)/shard_map/all_gather | solution.py:41
  77.1 286.2 %reduce-scatter.2.cloned.1.call-start = ((), (), s32[]{:S(2)}) async-start(), calls=%async_computation.4 | async-start | bytes 20054016 | tf_op jit(solution)/shard_map/reduce_scatter | solution.py:47
  366.7 8.3 %copy-start.1 = (s32[96,1]{0,1:T(1,128)S(1)}, s32[96,1]{0,1:T(1,128)}, u32[]{:S(2)}) copy-start(s32[96,1]{0,1:T(1,128)} %param.6) | copy-start | bytes 1156
  366.7 71.2 %all-to-all-start.1 = ((bf16[16,1,9,4096]{3,2,1,0:T(8,128)(2,1)}), bf16[16,1,9,4096]{3,2,1,0:T(8,128)(2,1)}, u32[]{:S(2)}, u32[]{:S(2)}) async-start(bf16[16,1,9,4096]{3,2,1,0:T(8,128)(2,1)} %copy.13), calls=%async_computation.2 | async-start | bytes 4194304 | tf_op jit(solution)/shard_map/all_to_all | solution.py:55
Sparse Core Ops, SparseCore 0:
  77.2 123.5 all-gather.1
  237.8 125.5 reduce-scatter.1
where the time goes:
time: 449 us
  waiting for transfers between devices  249 us (55%)
  blocking collectives  122 us (27%)
  matrix products  39.8 us (9%)
  between operations  15.9 us (4%)
  local copies, waits for them, and re-layouts  8.61 us (2%)
  starting transfers between devices  8.38 us (2%)
  other arithmetic  5.11 us (1%)
    reduce_scatter x1, waiting for transfers between devices, body(): lax.psum_scatter(jnp.einsum('secf,efd->secd', hidden, down_weight, prefer...  126 us
    all_gather x1, waiting for transfers between devices, body(): block_rows = lax.all_gather(received, GRP, axis=0, tiled=True)  124 us
    psum x4, blocking collectives, one_axis_at_a_time(): array = lax.psum(array, axis)  61 us
    all_to_all x1, blocking collectives, body(): lax.all_to_all(packed, EP, split_axis=0, concat_axis=0, tiled=True)  60.9 us
    dot_general x1, matrix products, body(): jnp.einsum('secf,efd->secd', hidden, down_weight, preferred_element_type=...  26.2 us
    dot_general x1, matrix products, body(): jnp.einsum('secd,edf->secf', block_rows, up_weight, preferred_element_typ...  10.6 us
  transfers between devices with their start and end apart: 3, of which 2 were waited for; matrix products, arithmetic and copies ran while one was open for 0% of the time, Pallas kernels for 0%

commit v1 on v0

--- a/solution.py
+++ b/solution.py
@@ -38,7 +38,8 @@
     packed = jnp.dot(placing, normed, preferred_element_type=jnp.float32).astype(jnp.bfloat16)
     packed = packed.reshape(ep_size, local_experts, capacity, model_width)
     received = lax.all_to_all(packed, EP, split_axis=0, concat_axis=0, tiled=True)
-    block_rows = lax.all_gather(received, GRP, axis=0, tiled=True)
+    outgoing = jnp.stack([received] * lax.axis_size(GRP))
+    block_rows = jnp.concatenate(lax.all_to_all(outgoing, GRP, 0, 0), axis=0)
     gate_out = jnp.einsum(
         "secd,edf->secf", block_rows, gate_weight, preferred_element_type=jnp.float32
     )

time: 449 us -> 542 us (1.21)
  blocking collectives: 122 us -> 338 us
  waiting for transfers between devices: 249 us -> 119 us
  local copies, waits for them, and re-layouts: 8.61 us -> 16.4 us
    all_to_all x0 -> x1, blocking collectives: none -> 216 us  [body(): block_rows = jnp.concatenate(lax.all_to_all(outgoing, GRP, 0, 0), axis=0)]
    all_gather x1 -> x0, waiting for transfers between devices: 124 us -> none  [body(): block_rows = lax.all_gather(received, GRP, axis=0, tiled=True)]
    reduce_scatter x1, waiting for transfers between devices: 126 us -> 119 us  [body(): lax.psum_scatter(jnp.einsum('secf,efd->secd', hidden, down_weight, prefer...]
    all_to_all x0 -> x1, local copies, waits for them, and re-layouts: none -> 6.6 us  [body(): block_rows = jnp.concatenate(lax.all_to_all(outgoing, GRP, 0, 0), axis=0)]
  transfers between devices with their start and end apart: 3 -> 2, of which waited for: 2 -> 1; matrix products, arithmetic and copies ran while one was open for 0% -> 0% of each run, Pallas kernels for 0% -> 0%
where the time goes in v1:
time: 542 us
  blocking collectives  338 us (62%)
  waiting for transfers between devices  119 us (22%)
  matrix products  39.5 us (7%)
  local copies, waits for them, and re-layouts  16.4 us (3%)
  between operations  15.9 us (3%)
  starting transfers between devices  8.31 us (2%)
    all_to_all x1, blocking collectives, body(): block_rows = jnp.concatenate(lax.all_to_all(outgoing, GRP, 0, 0), axis=0)  216 us
    reduce_scatter x1, waiting for transfers between devices, body(): lax.psum_scatter(jnp.einsum('secf,efd->secd', hidden, down_weight, prefer...  119 us
    psum x4, blocking collectives, one_axis_at_a_time(): array = lax.psum(array, axis)  61 us
    all_to_all x1, blocking collectives, body(): lax.all_to_all(packed, EP, split_axis=0, concat_axis=0, tiled=True)  60.9 us
    dot_general x1, matrix products, body(): jnp.einsum('secf,efd->secd', hidden, down_weight, preferred_element_type=...  26.1 us
  transfers between devices with their start and end apart: 2, of which 1 were waited for; matrix products, arithmetic and copies ran while one was open for 0% of the time, Pallas kernels for 0%

profile of v1, /device:TPU:1, one launch (start us, length us, event | category | flops | bytes accessed | tf_op | source)
XLA Modules:
  0.0 541.6 jit_solution(9462351243214822090)
XLA Ops:
  7.2 0.0 copy-start
  7.2 0.0 reduce-scatter.2.cloned.1.call-start
  7.2 0.9 fusion.21
  8.1 0.1 reduce_window_sum.11
  8.2 0.8 select_reduce_fusion
  9.1 0.7 multiply_add_fusion
  9.7 1.4 fusion.9
  11.2 1.7 convolution_convert_fusion
  12.8 1.6 reshape.58
  14.5 60.9 %all_to_all.22 = bf16[16,1,9,4096]{3,2,1,0:T(8,128)(2,1)S(1)} all-to-all(bf16[16,1,9,4096]{3,2,1,0:T(8,128)(2,1)} %bitcast.71), channel_id=1, replica_groups=mesh['grp_0'=4,'grp_1'=4,'ep_0'=8,'ep_1'=2] {'ep_0','ep_1'}, dimensions={0} | all-to-all | bytes 2359296 | tf_op jit(solution)/shard_map/all_to_all | solution.py:40
  75.3 0.7 copy.12
  76.1 2.2 stack.2
  78.3 216.1 %all_to_all.23 = bf16[16,16,1,9,4096]{4,1,3,2,0:T(8,128)(2,1)S(1)} all-to-all(bf16[16,16,1,9,4096]{4,1,3,2,0:T(8,128)(2,1)S(1)} %stack.2), channel_id=1, replica_groups=mesh['grp_0'=4,'grp_1'=4,'ep_0'=8,'ep_1'=2] {'grp_0','grp_1'}, dimensions={0} | all-to-all | bytes 37748736 | tf_op jit(solution)/shard_map/all_to_all | solution.py:42
  294.4 0.0 copy-start.2
  294.4 6.6 %copy.13 = bf16[16,16,1,9,4096]{4,1,0,3,2:T(8,128)(2,1)} copy(bf16[16,16,1,9,4096]{4,1,3,2,0:T(8,128)(2,1)S(1)} %all_to_all.23) | data formatting | bytes 37748736 | tf_op jit(solution)/shard_map/all_to_all | solution.py:42
  301.0 0.0 copy-done.2
  301.0 10.4 %fusion.5 = f32[256,9,256]{2,0,1:T(8,128)} fusion(bf16[256,9,4096]{2,0,1:T(8,128)(2,1)} %bitcast.69, bf16[1,4096,256]{2,1,0:T(8,128)(2,1)S(1)} %copy-done.2), kind=kOutput, calls=%fused_computation.11 | convolution fusion | flops 4831838208 | bytes 23330816 | tf_op jit(solution)/shard_map/secd,edf->secf/dot_general | solution.py:46
  311.3 0.0 copy-done
  311.3 26.1 %convert_bitcast_fusion = bf16[256,1,9,4096]{3,0,2,1:T(8,128)(2,1)} fusion(bf16[1,256,4096]{2,1,0:T(8,128)(2,1)S(1)} %copy-done, f32[256,9,256]{2,0,1:T(8,128)} %fusion.5, bf16[256,9,4096]{2,0,1:T(8,128)(2,1)} %bitcast.70, bf16[1,4096,256]{2,1,0:T(8,128)(2,1)} %param.7), kind=kOutput, calls=%fused_computation | convolution fusion | flops 9676652544 | bytes 44302336 | tf_op jit(solution)/shard_map/secf,efd->secd/dot_general | solution.py:49
  337.4 0.0 reduce-scatter.2.cloned.1.call-update
  337.5 118.5 %reduce-scatter.2.cloned.1.call-done = bf16[16,1,9,4096]{3,0,2,1:T(8,128)(2,1)} async-done(((bf16[256,1,9,4096]{3,0,2,1:T(8,128)(2,1)}), bf16[16,1,9,4096]{3,0,2,1:T(8,128)(2,1)}) %reduce-scatter.2.cloned.1.call-update) | async-done | bytes 1179664 | tf_op jit(solution)/shard_map/reduce_scatter | solution.py:48
  456.0 3.4 copy.14
  459.4 0.0 copy-start.1
  459.4 8.3 %all-to-all-start.2 = ((bf16[16,1,9,4096]{3,2,1,0:T(8,128)(2,1)}), bf16[16,1,9,4096]{3,2,1,0:T(8,128)(2,1)}, u32[]{:S(2)}, u32[]{:S(2)}) async-start(bf16[16,1,9,4096]{3,2,1,0:T(8,128)(2,1)} %copy.14), calls=%async_computation.3 | async-start | bytes 4194304 | tf_op jit(solution)/shard_map/all_to_all | solution.py:56
  467.7 0.0 copy-done.1
  467.7 0.1 convert_reduce_fusion
  467.8 8.8 %psum.28 = f32[16]{0:T(128)S(1)} all-reduce(f32[16]{0:T(128)S(1)} %convert_reduce_fusion), channel_id=1, replica_groups=mesh['grp_0'=4,'grp_1'=4,'ep_0'=8,'ep_1'=2] {'grp_0'}, use_global_device_ids=true, to_apply=%region_5.6 | all-reduce | flops 16 | bytes 128 | tf_op jit(solution)/shard_map/psum | solution.py:15
  476.5 7.4 %psum.29 = f32[16]{0:T(128)S(1)} all-reduce(f32[16]{0:T(128)S(1)} %psum.28), channel_id=1, replica_groups=mesh['grp_0'=4,'grp_1'=4,'ep_0'=8,'ep_1'=2] {'grp_1'}, use_global_device_ids=true, to_apply=%region_6.7 | all-reduce | flops 16 | bytes 128 | tf_op jit(solution)/shard_map/psum | solution.py:15
  483.9 39.3 %psum.30 = f32[16]{0:T(128)S(1)} all-reduce(f32[16]{0:T(128)S(1)} %psum.29), channel_id=1, replica_groups=mesh['grp_0'=4,'grp_1'=4,'ep_0'=8,'ep_1'=2] {'ep_0'}, use_global_device_ids=true, to_apply=%region_7.8 | all-reduce | flops 16 | bytes 128 | tf_op jit(solution)/shard_map/psum | solution.py:15
  523.2 5.5 %psum.31 = f32[16]{0:T(128)S(1)} all-reduce(f32[16]{0:T(128)S(1)} %psum.30), channel_id=1, replica_groups=mesh['grp_0'=4,'grp_1'=4,'ep_0'=8,'ep_1'=2] {'ep_1'}, use_global_device_ids=true, to_apply=%region_8.9 | all-reduce | flops 16 | bytes 128 | tf_op jit(solution)/shard_map/psum | solution.py:15
  528.8 1.1 multiply_reduce_fusion
  530.5 0.0 all-to-all-done.2
  530.5 1.8 reshape.64
  532.4 1.3 convolution_convert_fusion.1
  (1 shorter events, 0.0 us)
Async XLA Ops:
  7.2 304.2 %copy-start = (bf16[1,256,4096]{2,1,0:T(8,128)(2,1)S(1)}, bf16[1,256,4096]{2,1,0:T(8,128)(2,1)}, u32[]{:S(2)}) copy-start(bf16[1,256,4096]{2,1,0:T(8,128)(2,1)} %param.9) | copy-start | bytes 6291460
  7.2 448.8 %reduce-scatter.2.cloned.1.call-start = ((), (), s32[]{:S(2)}) async-start(), calls=%async_computation.4 | async-start | bytes 20054016 | tf_op jit(solution)/shard_map/reduce_scatter | solution.py:48
  294.4 6.6 %copy-start.2 = (bf16[1,4096,256]{2,1,0:T(8,128)(2,1)S(1)}, bf16[1,4096,256]{2,1,0:T(8,128)(2,1)}, u32[]{:S(2)}) copy-start(bf16[1,4096,256]{2,1,0:T(8,128)(2,1)} %param.8) | copy-start | bytes 6291460
  459.4 8.3 %copy-start.1 = (s32[96,1]{0,1:T(1,128)S(1)}, s32[96,1]{0,1:T(1,128)}, u32[]{:S(2)}) copy-start(s32[96,1]{0,1:T(1,128)} %param.6) | copy-start | bytes 1156
  459.4 71.1 %all-to-all-start.2 = ((bf16[16,1,9,4096]{3,2,1,0:T(8,128)(2,1)}), bf16[16,1,9,4096]{3,2,1,0:T(8,128)(2,1)}, u32[]{:S(2)}, u32[]{:S(2)}) async-start(bf16[16,1,9,4096]{3,2,1,0:T(8,128)(2,1)} %copy.14), calls=%async_computation.3 | async-start | bytes 4194304 | tf_op jit(solution)/shard_map/all_to_all | solution.py:56
Sparse Core Ops, SparseCore 0:
  337.6 118.3 reduce-scatter.1
